TPU v7x, 32 devices: a whole 2x2x4 slice. The times are simulated.
32 devices in a mesh: row: 4 (over y, core), col: 8 (over z, x).
Axes of the slice: x: 2, y: 2, z: 4, core: 2. Of those that a mesh axis runs over, the one named last changes fastest.
Arguments:
- velocity_modes: bfloat16 [3, 176, 352, 704], P(None, 'row', 'col'), may hold values from -0.00090789795 to 0.00090789795
- wavenumbers: float32 [8], replicated, may hold values from 0.5 to 3
- polar: float32 [8], replicated, may hold values from -3.140625 to 3.140625
- azimuth: float32 [8], replicated, may hold values from -3.140625 to 3.140625
Outputs:
- velocity: bfloat16 [3, 512, 512, 512], P(None, 'row', 'col')
- far_field: float32 [8, 2, 8], P('col')
All inputs are finite; a program needn't handle non-finite values.
Results may differ from a plain program's by a relative error of at most 0.0075.
Values may be sent and summed in bfloat16 or wider, within the bound.
A program may use at most 192 MiB of HBM per device.

v0:
```python
import math
import jax
import jax.numpy as jnp
from jax import lax
from jax.sharding import PartitionSpec as P

N = 512
M = 352
KX = 176
FREQS = 8


def complex_table(modes, points):
    waves = jnp.arange(modes, dtype=jnp.int32) - modes // 2
    cells = jnp.arange(points, dtype=jnp.int32)
    product = jnp.mod(waves[:, None] * cells[None, :], points)
    angle = product.astype(jnp.float32) * (2.0 * math.pi / points)
    cosine = jnp.cos(angle)
    sine = jnp.sin(angle)
    table = jnp.stack([jnp.stack([cosine, sine], 1), jnp.stack([-sine, cosine], 1)], 0)
    return table.astype(jnp.bfloat16)


def half_table(count, points):
    waves = jnp.arange(count, dtype=jnp.int32)
    cells = jnp.arange(points, dtype=jnp.int32)
    product = jnp.mod(waves[:, None] * cells[None, :], points)
    angle = product.astype(jnp.float32) * (2.0 * math.pi / points)
    cosine = jnp.cos(angle).astype(jnp.bfloat16)
    sine = jnp.sin(angle).astype(jnp.bfloat16)
    factor = jnp.where(waves == 0, 1.0, 2.0).astype(jnp.bfloat16)[:, None]
    return jnp.stack([factor * cosine, -(factor * sine)], 0)


def stresses(field):
    trace = (field[0] * field[0] + field[1] * field[1] + field[2] * field[2]) / 3.0
    parts = [
        field[0] * field[0] - trace,
        field[1] * field[1] - trace,
        field[2] * field[2] - trace,
        field[0] * field[1],
        field[0] * field[2],
        field[1] * field[2],
    ]
    return jnp.stack(parts, 0).astype(jnp.bfloat16)


def far_terms(stress, wave_j, axis_one, axis_two, axis_three, y_pos, z_pos):
    points = stress.shape[-1]
    y_count = stress.shape[1]
    z_count = stress.shape[2]
    count = wave_j.shape[0]
    x_pos = jnp.arange(points, dtype=jnp.int32).astype(jnp.float32) * (2.0 * math.pi / points)
    angle_x = wave_j[None, :] * (axis_one[None, :] * x_pos[:, None])
    phase_x = (
        jnp.stack([jnp.cos(angle_x), -jnp.sin(angle_x)], 1)
        .reshape(points, 2 * count)
        .astype(jnp.bfloat16)
    )
    lines = jnp.dot(
        stress.reshape(6 * y_count * z_count, points), phase_x, preferred_element_type=jnp.float32
    )
    lines = lines.reshape(6, y_count, z_count, 2, count)
    weights = [
        axis_one * axis_one,
        axis_two * axis_two,
        axis_three * axis_three,
        2.0 * axis_one * axis_two,
        2.0 * axis_one * axis_three,
        2.0 * axis_two * axis_three,
    ]
    mixed = weights[0][None, None, None, :] * lines[0]
    for index in range(1, 6):
        mixed = mixed + weights[index][None, None, None, :] * lines[index]
    angle = wave_j[None, None, :] * (axis_two[None, None, :] * y_pos[:, None, None]) + wave_j[
        None, None, :
    ] * (axis_three[None, None, :] * z_pos[None, :, None])
    cosine = jnp.cos(angle)
    sine = jnp.sin(angle)
    real_part = mixed[:, :, 0, :]
    imag_part = mixed[:, :, 1, :]
    return jnp.stack(
        [
            jnp.sum(real_part * cosine + imag_part * sine, (0, 1)),
            jnp.sum(imag_part * cosine - real_part * sine, (0, 1)),
        ],
        0,
    )


def body(velocity_modes, wavenumbers, polar, azimuth):
    table = complex_table(M, N)
    table_x = half_table(KX, N)
    rows_kx = velocity_modes.shape[1]
    cols_ky = velocity_modes.shape[2]
    modes = velocity_modes.reshape(3, rows_kx, cols_ky, 2, M)
    first = jnp.einsum(
        "cabpk,pkqz->caqbz", modes, table, preferred_element_type=jnp.float32
    ).astype(jnp.bfloat16)
    moved = lax.all_to_all(first, "col", split_axis=4, concat_axis=3, tiled=True)
    second = jnp.einsum(
        "caqbz,qbpy->cazpy", moved, table, preferred_element_type=jnp.float32
    ).astype(jnp.bfloat16)
    arrived = lax.all_to_all(second, "row", split_axis=4, concat_axis=1, tiled=True)
    field = jnp.einsum("cazpy,pax->cyzx", arrived, table_x, preferred_element_type=jnp.float32)
    velocity = field.astype(jnp.bfloat16)
    stress = stresses(field)
    y_local = field.shape[1]
    z_local = field.shape[2]
    dirs = polar.shape[0]
    wave_j = jnp.repeat(wavenumbers, dirs)
    axis_one = jnp.tile(jnp.sin(polar) * jnp.cos(azimuth), FREQS)
    axis_two = jnp.tile(jnp.sin(polar) * jnp.sin(azimuth), FREQS)
    axis_three = jnp.tile(jnp.cos(polar), FREQS)
    y_index = lax.axis_index("row") * y_local + jnp.arange(y_local, dtype=jnp.int32)
    z_index = lax.axis_index("col") * z_local + jnp.arange(z_local, dtype=jnp.int32)
    y_pos = y_index.astype(jnp.float32) * (2.0 * math.pi / N)
    z_pos = z_index.astype(jnp.float32) * (2.0 * math.pi / N)
    terms = far_terms(stress, wave_j, axis_one, axis_two, axis_three, y_pos, z_pos)
    spectrum = terms.reshape(2, FREQS, dirs) * (wavenumbers * wavenumbers)[None, :, None] / N**1.5
    partial_sum = jnp.transpose(spectrum, (2, 0, 1))
    owned = lax.psum_scatter(partial_sum, "col", scatter_dimension=0, tiled=True)
    far_field = lax.psum(owned, "row")
    return (velocity, far_field)


def solution(mesh):
    return jax.shard_map(
        body,
        mesh=mesh,
        in_specs=(P(None, "row", "col", None), P(), P(), P()),
        out_specs=(P(None, "row", "col", None), P("col", None, None)),
        check_vma=False,
    )
```

profile of v0, /device:TPU:0, one launch (start us, length us, event | category | flops | bytes accessed | tf_op | source)
XLA Modules:
  0.0 1565.9 jit_solution(17726658873091997270)
XLA Ops:
  0.6 20.4 %reshape.626 = bf16[3,44,44,2,352]{4,3,2,1,0:T(2,128)(2,1)} reshape(bf16[3,44,44,704]{3,2,1,0:T(8,128)(2,1)} %param.4) | data formatting | bytes 16355328 | tf_op jit(solution)/shard_map/reshape | solution.py:96
  24.4 17.3 %fusion.7 = bf16[3,44,2,44,512]{4,3,1,0,2:T(8,128)(2,1)} fusion(bf16[3,44,44,2,352]{4,3,2,1,0:T(2,128)(2,1)} %reshape.626, bf16[1,352,2,512]{3,1,0,2:T(8,128)(2,1)S(1)} %get-tuple-element.23, bf16[1,352,2,512]{3,1,0,2:T(8,128)(2,1)S(1)} %get-tuple-element.22), kind=kOutput, calls=%fused_computation.16 | convolution fusion | flops 8382758912 | bytes 21514240 | tf_op jit(solution)/shard_map/cabpk,pkqz->caqbz/dot_general | solution.py:97
  41.7 70.2 %copy.64 = bf16[3,44,2,44,512]{3,2,1,0,4:T(2,128)(2,1)} copy(bf16[3,44,2,44,512]{4,3,1,0,2:T(8,128)(2,1)} %fusion.7) | data formatting | bytes 23789568 | tf_op jit(solution)/shard_map/convert_element_type | solution.py:99
  111.9 118.5 %reshape.636 = bf16[8,2,371712]{2,1,0:T(2,128)(2,1)} reshape(bf16[512,3,44,2,44]{4,3,2,1,0:T(2,128)(2,1)} %bitcast.97) | data formatting | bytes 23789568
  230.3 267.3 %all_to_all.36 = bf16[8,2,371712]{2,1,0:T(2,128)(2,1)} all-to-all(bf16[8,2,371712]{2,1,0:T(2,128)(2,1)} %reshape.636), channel_id=1, replica_groups=mesh['row'=4,'col'=8] {'col'}, dimensions={0} | all-to-all | bytes 23789568 | tf_op jit(solution)/shard_map/all_to_all | solution.py:100
  497.6 126.0 %reshape.637 = bf16[512,3,44,2,44]{4,3,2,1,0:T(2,128)(2,1)} reshape(bf16[8,2,371712]{2,1,0:T(2,128)(2,1)} %all_to_all.36) | data formatting | bytes 23789568
  623.6 23.6 %copy.101 = bf16[3,44,2,44,8,64]{3,4,5,2,1,0:T(8,128)(2,1)} copy(bf16[3,44,2,44,8,64]{3,2,1,0,5,4:T(2,128)(2,1)} %bitcast.98) | data formatting | bytes 23789568 | tf_op jit(solution)/shard_map/all_to_all | solution.py:100
  647.2 44.0 %reshape.630 = bf16[3,44,2,352,64,1]{3,4,2,1,0,5:T(8,128)(2,1)} reshape(bf16[3,44,2,8,44,64]{4,3,5,2,1,0:T(8,128)(2,1)} %bitcast.99) | data formatting | bytes 23789568 | tf_op jit(solution)/shard_map/all_to_all | solution.py:100
  691.2 21.6 %bitcast_convert_fusion = bf16[3,44,64,2,512]{4,2,3,1,0:T(8,128)(2,1)} fusion(bf16[3,44,2,352,64,1]{3,4,2,1,0,5:T(8,128)(2,1)} %reshape.630, bf16[1,352,2,512]{3,1,0,2:T(8,128)(2,1)S(1)} %get-tuple-element.23, bf16[1,352,2,512]{3,1,0,2:T(8,128)(2,1)S(1)} %get-tuple-element.22), kind=kOutput, calls=%fused_computation | convolution fusion | flops 12191793152 | bytes 30638080 | tf_op jit(solution)/shard_map/caqbz,qbpy->cazpy/dot_general | solution.py:101
  712.9 69.9 %copy.67 = bf16[3,44,64,2,512]{2,3,1,0,4:T(2,128)(2,1)} copy(bf16[3,44,64,2,512]{4,2,3,1,0:T(8,128)(2,1)} %bitcast_convert_fusion) | data formatting | bytes 34603008 | tf_op jit(solution)/shard_map/convert_element_type | solution.py:103
  782.7 48.9 %reshape.638 = bf16[4,2,1081344]{2,1,0:T(2,128)(2,1)} reshape(bf16[512,3,44,2,64]{4,3,2,1,0:T(2,128)(2,1)} %bitcast.95) | data formatting | bytes 34603008
  845.7 182.1 %all-to-all-done.1 = bf16[4,2,1081344]{2,1,0:T(2,128)(2,1)} async-done(((bf16[4,2,1081344]{2,1,0:T(2,128)(2,1)}), bf16[4,2,1081344]{2,1,0:T(2,128)(2,1)}, u32[]{:S(2)}, u32[]{:S(2)}) %all-to-all-start.1) | async-done | bytes 17301536 | tf_op jit(solution)/shard_map/all_to_all | solution.py:104
  1027.8 47.9 %reshape.639 = bf16[512,3,44,2,64]{4,3,2,1,0:T(2,128)(2,1)} reshape(bf16[4,2,1081344]{2,1,0:T(2,128)(2,1)} %all-to-all-done.1) | data formatting | bytes 34603008
  1075.7 83.6 %copy.89 = bf16[3,44,64,2,4,128]{5,4,2,3,1,0:T(4,128)(2,1)} copy(bf16[3,44,64,2,4,128]{2,3,1,0,5,4:T(2,128)(2,1)} %bitcast.96) | data formatting | bytes 34603008 | tf_op jit(solution)/shard_map/all_to_all | solution.py:104
  1159.3 15.6 copy.69
  1174.8 33.4 %fusion.53 = (bf16[3,128,64,512]{3,1,2,0:T(8,128)(2,1)}, f32[3,128,64,512]{3,1,2,0:T(8,128)}) fusion(bf16[3,176,64,2,128]{4,2,3,1,0:T(8,128)(2,1)} %bitcast.100, bf16[1,176,512]{2,1,0:T(8,128)(2,1)S(1)} %get-tuple-element.42, bf16[1,176,512]{2,1,0:T(8,128)(2,1)S(1)} %get-tuple-element.41), kind=kOutput, calls=%fused_computation.97 | convolution fusion | flops 8871673856 | bytes 93159424 | tf_op jit(solution)/shard_map/cazpy,pax->cyzx/dot_general | solution.py:105
  1208.3 26.8 %copy.79 = bf16[3,128,64,512]{3,2,1,0:T(8,128)(2,1)} copy(bf16[3,128,64,512]{3,1,2,0:T(8,128)(2,1)} %get-tuple-element.43) | data formatting | bytes 50331648
  1235.1 20.9 %fusion.10 = (bf16[6,128,64,512]{3,1,2,0:T(8,128)(2,1)}, f32[1,128,64,512]{3,1,2,0:T(8,128)S(1)}) fusion(f32[3,128,64,512]{3,1,2,0:T(8,128)} %get-tuple-element.44), kind=kLoop, calls=%fused_computation.17 | loop fusion | flops 33554432 | bytes 75497472
  1255.9 10.9 fusion.11
  1266.9 11.0 fusion.12
  1277.8 15.0 fusion.13
  1292.9 15.1 fusion.14
  1308.0 15.1 fusion.15
  1323.0 45.4 %copy.71 = bf16[6,128,64,512]{3,2,1,0:T(8,128)(2,1)} copy(bf16[6,128,64,512]{3,1,2,0:T(8,128)(2,1)} %fusion.15) | data formatting | bytes 100663296 | tf_op jit(solution)/shard_map/stack | solution.py:45
  1368.5 30.4 %fusion.54 = f32[49152,128]{1,0:T(8,128)} fusion(bf16[49152,512]{1,0:T(8,128)(2,1)} %bitcast.94, bf16[512,128]{0,1:T(8,128)(2,1)S(1)} %bitcast.102), kind=kOutput, calls=%fused_computation.98 | convolution fusion | flops 6442450944 | bytes 75628544 | tf_op jit(solution)/shard_map/dot_general | solution.py:60
  1398.8 17.2 %fusion.51 = (f32[8192,128]{1,0:T(8,128)}, f32[8192,128]{1,0:T(8,128)}, f32[8192,128]{1,0:T(8,128)}, f32[8192,128]{1,0:T(8,128)}, f32[8192,128]{1,0:T(8,128)}, /*index=5*/f32[8192,128]{1,0:T(8,128)}) fusion(f32[49152,128]{1,0:T(8,128)} %fusion.54), kind=kLoop, calls=%fused_computation.95 | loop fusion | bytes 50331648 | tf_op jit(solution)/shard_map/slice | solution.py:72
  1421.6 7.9 squeeze.21
  1448.5 7.9 squeeze.19
  1475.5 7.9 squeeze.17
  1497.0 22.6 %multiply_add_fusion = f32[128,64,2,64]{1,0,3,2:T(8,128)} fusion(f32[128,64,2,64]{1,0,3,2:T(8,128)} %squeeze.21, f32[128,64,2,64]{1,0,3,2:T(8,128)} %squeeze.20, f32[128,64,2,64]{1,0,3,2:T(8,128)} %squeeze.19, f32[128,64,2,64]{1,0,3,2:T(8,128)} %squeeze.18, f32[128,64,2,64]{1,0,3,2:T(8,128)} %squeeze.17, f32[128,64,2,64]{1,0,3,2:T(8,128)} %squeeze.16, ...), kind=kLoop, calls=%fused_computation.23 | loop fusion | flops 11534336 | bytes 29361664 | tf_op jit(solution)/shard_map/add | solution.py:74
  1519.7 19.8 %fusion.21 = (f32[64]{0:T(128)S(1)}, f32[64]{0:T(128)S(1)}) fusion(f32[128,64,2,64]{1,0,3,2:T(8,128)} %multiply_add_fusion, f32[64,64]{0,1:T(8,128)S(1)} %copy-done.1, f32[128,64]{0,1:T(8,128)S(1)} %copy-done.2), kind=kLoop, calls=%fused_computation.31 | loop fusion | flops 4718464 | bytes 4243968 | tf_op jit(solution)/shard_map/reduce_sum | solution.py:84
  1539.8 19.0 %all-reduce = f32[8,2,8]{2,1,0:T(2,128)S(1)} all-reduce(f32[8,2,8]{2,1,0:T(2,128)S(1)} %copy.78), channel_id=2, replica_groups=mesh['row'=4,'col'=8] {'col'}, use_global_device_ids=true, to_apply=%region_2.3.clone | all-reduce | flops 128 | bytes 1024
  (69 shorter events, 82.0 us)
Async XLA Ops:
  831.7 7.5 copy-start.12
  831.7 7.6 copy-start.11
  831.7 7.7 copy-start.9
  831.7 8.6 copy-start.13
  831.7 196.1 %all-to-all-start.1 = ((bf16[4,2,1081344]{2,1,0:T(2,128)(2,1)}), bf16[4,2,1081344]{2,1,0:T(2,128)(2,1)}, u32[]{:S(2)}, u32[]{:S(2)}) async-start(bf16[4,2,1081344]{2,1,0:T(2,128)(2,1)} %reshape.638), calls=%async_computation.1 | async-start | bytes 34603008 | tf_op jit(solution)/shard_map/all_to_all | solution.py:104
  1323.0 45.4 %copy-start = (bf16[512,2,64]{0,2,1:T(8,128)(2,1)S(1)}, bf16[512,2,64]{0,2,1:T(8,128)(2,1)}, u32[]{:S(2)}) copy-start(bf16[512,2,64]{0,2,1:T(8,128)(2,1)} %pad_maximum_fusion.3) | copy-start | bytes 393220
  1483.3 13.7 copy-start.3
  1483.3 13.7 copy-start.4
  1483.3 13.7 copy-start.5
  1483.3 13.7 copy-start.6
  1483.3 13.7 copy-start.7
  1483.3 13.7 copy-start.8
  1497.0 22.7 %copy-start.1 = (f32[64,64]{0,1:T(8,128)S(1)}, f32[64,64]{0,1:T(8,128)}, u32[]{:S(2)}) copy-start(f32[64,64]{0,1:T(8,128)} %multiply_multiply_fusion.1) | copy-start | bytes 49156
  1497.0 22.7 %copy-start.2 = (f32[128,64]{0,1:T(8,128)S(1)}, f32[128,64]{0,1:T(8,128)}, u32[]{:S(2)}) copy-start(f32[128,64]{0,1:T(8,128)} %multiply_multiply_fusion.2) | copy-start | bytes 98308
  1497.0 42.6 %copy-start.10 = (f32[8]{0:T(128)S(1)}, f32[8]{0:T(128)}, u32[]{:S(2)}) copy-start(f32[8]{0:T(128)} %mul.534) | copy-start | bytes 100
where the time goes:
time: 1580 us; the launch traced here: 1570 us
  local copies, waits for them, and re-layouts  841 us (53%)
  blocking collectives  293 us (19%)
  waiting for transfers between devices  182 us (12%)
  other arithmetic  139 us (9%)
  matrix products  103 us (7%)
    unnamed x35, local copies, waits for them, and re-layouts  369 us
    all_to_all x1, blocking collectives, body(): lax.all_to_all(first, 'col', split_axis=4, concat_axis=3, tiled=True)  267 us
    all_to_all x1, waiting for transfers between devices, body(): lax.all_to_all(second, 'row', split_axis=4, concat_axis=1, tiled=True)  182 us
    all_to_all x2, local copies, waits for them, and re-layouts, body(): lax.all_to_all(second, 'row', split_axis=4, concat_axis=1, tiled=True)  99.1 us
    unnamed x5, other arithmetic  72.9 us
    convert_element_type x1, local copies, waits for them, and re-layouts, body(): first = jnp.einsum('cabpk,pkqz->caqbz', modes, table, preferred_element_t...  70.2 us
    convert_element_type x1, local copies, waits for them, and re-layouts, body(): second = jnp.einsum('caqbz,qbpy->cazpy', moved, table, preferred_element_...  69.9 us
    all_to_all x2, local copies, waits for them, and re-layouts, body(): lax.all_to_all(first, 'col', split_axis=4, concat_axis=3, tiled=True)  67.6 us
  transfers between devices with their start and end apart: 1, of which 1 were waited for; matrix products, arithmetic and copies ran while one was open for 0% of the time, Pallas kernels for 0%

commit v1 on v0

--- a/solution.py
+++ b/solution.py
@@ -101,7 +101,10 @@
     second = jnp.einsum(
         "caqbz,qbpy->cazpy", moved, table, preferred_element_type=jnp.float32
     ).astype(jnp.bfloat16)
-    arrived = lax.all_to_all(second, "row", split_axis=4, concat_axis=1, tiled=True)
+    arrived = jnp.concatenate(
+        lax.all_to_all(jnp.stack(jnp.split(second, lax.axis_size("row"), axis=4)), "row", 0, 0),
+        axis=1,
+    )
     field = jnp.einsum("cazpy,pax->cyzx", arrived, table_x, preferred_element_type=jnp.float32)
     velocity = field.astype(jnp.bfloat16)
     stress = stresses(field)

time: 1580 us -> 1340 us (0.85)
  local copies, waits for them, and re-layouts: 841 us -> 600 us
    all_to_all x2 -> x0, local copies, waits for them, and re-layouts: 99.1 us -> none  [body(): lax.all_to_all(second, 'row', split_axis=4, concat_axis=1, tiled=True)]
    unnamed x35 -> x33, local copies, waits for them, and re-layouts: 369 us -> 272 us
    convert_element_type x1 -> x0, local copies, waits for them, and re-layouts: 69.9 us -> none  [body(): second = jnp.einsum('caqbz,qbpy->cazpy', moved, table, preferred_element_...]
    reshape x0 -> x1, local copies, waits for them, and re-layouts: none -> 16.4 us  [body(): jnp.concatenate(lax.all_to_all(jnp.stack(jnp.split(second, lax.axis_size(...]
where the time goes in v1:
time: 1340 us; the launch traced here: 1330 us
  local copies, waits for them, and re-layouts  600 us (45%)
  blocking collectives  293 us (22%)
  waiting for transfers between devices  182 us (14%)
  other arithmetic  147 us (11%)
  matrix products  102 us (8%)
    unnamed x33, local copies, waits for them, and re-layouts  272 us
    all_to_all x1, blocking collectives, body(): lax.all_to_all(first, 'col', split_axis=4, concat_axis=3, tiled=True)  268 us
    all_to_all x1, waiting for transfers between devices, body(): lax.all_to_all(jnp.stack(jnp.split(second, lax.axis_size('row'), axis=4))...  182 us
    unnamed x5, other arithmetic  73.1 us
    convert_element_type x1, local copies, waits for them, and re-layouts, body(): first = jnp.einsum('cabpk,pkqz->caqbz', modes, table, preferred_element_t...  70.1 us
    all_to_all x2, local copies, waits for them, and re-layouts, body(): lax.all_to_all(first, 'col', split_axis=4, concat_axis=3, tiled=True)  67.6 us
    another operation x1, local copies, waits for them, and re-layouts, stresses(): return jnp.stack(parts, 0).astype(jnp.bfloat16)  45.5 us
    squeeze x5, local copies, waits for them, and re-layouts, far_terms(): mixed = mixed + weights[index][None, None, None, :] * lines[index]  39.5 us
  transfers between devices with their start and end apart: 1, of which 1 were waited for; matrix products, arithmetic and copies ran while one was open for 0% of the time, Pallas kernels for 0%

profile of v1, /device:TPU:0, one launch (start us, length us, event | category | flops | bytes accessed | tf_op | source)
XLA Modules:
  0.0 1331.8 jit_solution(10194990814005087646)
XLA Ops:
  0.6 20.4 %reshape.632 = bf16[3,44,44,2,352]{4,3,2,1,0:T(2,128)(2,1)} reshape(bf16[3,44,44,704]{3,2,1,0:T(8,128)(2,1)} %param.4) | data formatting | bytes 16355328 | tf_op jit(solution)/shard_map/reshape | solution.py:96
  24.4 17.3 %fusion.7 = bf16[3,44,2,44,512]{4,3,1,0,2:T(8,128)(2,1)} fusion(bf16[3,44,44,2,352]{4,3,2,1,0:T(2,128)(2,1)} %reshape.632, bf16[1,352,2,512]{3,1,0,2:T(8,128)(2,1)S(1)} %get-tuple-element.25, bf16[1,352,2,512]{3,1,0,2:T(8,128)(2,1)S(1)} %get-tuple-element.24), kind=kOutput, calls=%fused_computation.17 | convolution fusion | flops 8382758912 | bytes 21514240 | tf_op jit(solution)/shard_map/cabpk,pkqz->caqbz/dot_general | solution.py:97
  41.7 70.1 %copy.45 = bf16[3,44,2,44,512]{3,2,1,0,4:T(2,128)(2,1)} copy(bf16[3,44,2,44,512]{4,3,1,0,2:T(8,128)(2,1)} %fusion.7) | data formatting | bytes 23789568 | tf_op jit(solution)/shard_map/convert_element_type | solution.py:99
  111.8 118.5 %reshape.644 = bf16[8,2,371712]{2,1,0:T(2,128)(2,1)} reshape(bf16[512,3,44,2,44]{4,3,2,1,0:T(2,128)(2,1)} %bitcast.100) | data formatting | bytes 23789568
  230.3 267.5 %all_to_all.23 = bf16[8,2,371712]{2,1,0:T(2,128)(2,1)} all-to-all(bf16[8,2,371712]{2,1,0:T(2,128)(2,1)} %reshape.644), channel_id=1, replica_groups=mesh['row'=4,'col'=8] {'col'}, dimensions={0} | all-to-all | bytes 23789568 | tf_op jit(solution)/shard_map/all_to_all | solution.py:100
  497.8 126.0 %reshape.645 = bf16[512,3,44,2,44]{4,3,2,1,0:T(2,128)(2,1)} reshape(bf16[8,2,371712]{2,1,0:T(2,128)(2,1)} %all_to_all.23) | data formatting | bytes 23789568
  623.8 23.6 %copy.79 = bf16[3,44,2,44,8,64]{3,4,5,2,1,0:T(8,128)(2,1)} copy(bf16[3,44,2,44,8,64]{3,2,1,0,5,4:T(2,128)(2,1)} %bitcast.101) | data formatting | bytes 23789568 | tf_op jit(solution)/shard_map/all_to_all | solution.py:100
  647.4 44.0 %reshape.638 = bf16[3,44,2,352,64,1]{3,4,2,1,0,5:T(8,128)(2,1)} reshape(bf16[3,44,2,8,44,64]{4,3,5,2,1,0:T(8,128)(2,1)} %bitcast.102) | data formatting | bytes 23789568 | tf_op jit(solution)/shard_map/all_to_all | solution.py:100
  691.4 21.2 %bitcast_convert_fusion = bf16[3,44,64,2,512]{4,2,3,1,0:T(8,128)(2,1)} fusion(bf16[3,44,2,352,64,1]{3,4,2,1,0,5:T(8,128)(2,1)} %reshape.638, bf16[1,352,2,512]{3,1,0,2:T(8,128)(2,1)S(1)} %get-tuple-element.25, bf16[1,352,2,512]{3,1,0,2:T(8,128)(2,1)S(1)} %get-tuple-element.24), kind=kOutput, calls=%fused_computation | convolution fusion | flops 12191793152 | bytes 30638080 | tf_op jit(solution)/shard_map/caqbz,qbpy->cazpy/dot_general | solution.py:101
  712.6 8.3 slice_bitcast_fusion.3
  742.0 182.2 %all-to-all-done.1 = bf16[4,3,44,64,2,128]{5,3,4,2,1,0:T(8,128)(2,1)} async-done(((bf16[4,3,44,64,2,128]{5,3,4,2,1,0:T(8,128)(2,1)}), bf16[4,3,44,64,2,128]{5,3,4,2,1,0:T(8,128)(2,1)}, u32[]{:S(2)}, u32[]{:S(2)}) %all-to-all-start.1) | async-done | bytes 17301536 | tf_op jit(solution)/shard_map/all_to_all | solution.py:105
  924.1 16.4 %copy.48 = bf16[3,4,44,64,2,128]{5,3,4,2,1,0:T(8,128)(2,1)} copy(bf16[3,4,44,64,2,128]{5,3,4,2,0,1:T(8,128)(2,1)} %bitcast.22) | data formatting | bytes 34603008 | tf_op jit(solution)/shard_map/reshape | solution.py:104
  940.5 33.4 %fusion.53 = (bf16[3,128,64,512]{3,1,2,0:T(8,128)(2,1)}, f32[3,128,64,512]{3,1,2,0:T(8,128)}) fusion(bf16[3,176,64,2,128]{4,2,3,1,0:T(8,128)(2,1)} %bitcast.103, bf16[1,176,512]{2,1,0:T(8,128)(2,1)S(1)} %get-tuple-element.44, bf16[1,176,512]{2,1,0:T(8,128)(2,1)S(1)} %get-tuple-element.43), kind=kOutput, calls=%fused_computation.102 | convolution fusion | flops 8871673856 | bytes 93159424 | tf_op jit(solution)/shard_map/cazpy,pax->cyzx/dot_general | solution.py:108
  974.0 26.6 %copy.58 = bf16[3,128,64,512]{3,2,1,0:T(8,128)(2,1)} copy(bf16[3,128,64,512]{3,1,2,0:T(8,128)(2,1)} %get-tuple-element.45) | data formatting | bytes 50331648
  1000.6 20.9 %fusion.10 = (bf16[6,128,64,512]{3,1,2,0:T(8,128)(2,1)}, f32[1,128,64,512]{3,1,2,0:T(8,128)S(1)}) fusion(f32[3,128,64,512]{3,1,2,0:T(8,128)} %get-tuple-element.46), kind=kLoop, calls=%fused_computation.18 | loop fusion | flops 33554432 | bytes 75497472
  1021.5 10.9 fusion.11
  1032.4 11.2 fusion.12
  1043.5 15.1 %fusion.13 = bf16[6,128,64,512]{3,1,2,0:T(8,128)(2,1)} fusion(bf16[6,128,64,512]{3,1,2,0:T(8,128)(2,1)} %fusion.12, f32[3,128,64,512]{3,1,2,0:T(8,128)} %get-tuple-element.46), kind=kLoop, calls=%fused_computation.21 | loop fusion | flops 8388608 | bytes 41943040
  1058.6 15.1 %fusion.14 = bf16[6,128,64,512]{3,1,2,0:T(8,128)(2,1)} fusion(bf16[6,128,64,512]{3,1,2,0:T(8,128)(2,1)} %fusion.13, f32[3,128,64,512]{3,1,2,0:T(8,128)} %get-tuple-element.46), kind=kLoop, calls=%fused_computation.22 | loop fusion | flops 8388608 | bytes 41943040
  1073.7 15.1 %fusion.15 = bf16[6,128,64,512]{3,1,2,0:T(8,128)(2,1)} fusion(bf16[6,128,64,512]{3,1,2,0:T(8,128)(2,1)} %fusion.14, f32[3,128,64,512]{3,1,2,0:T(8,128)} %get-tuple-element.46), kind=kLoop, calls=%fused_computation.23 | loop fusion | flops 8388608 | bytes 41943040 | tf_op jit(solution)/shard_map/stack | solution.py:45
  1088.7 45.5 %copy.50 = bf16[6,128,64,512]{3,2,1,0:T(8,128)(2,1)} copy(bf16[6,128,64,512]{3,1,2,0:T(8,128)(2,1)} %fusion.15) | data formatting | bytes 100663296 | tf_op jit(solution)/shard_map/stack | solution.py:45
  1134.2 30.0 %fusion.54 = f32[49152,128]{1,0:T(8,128)} fusion(bf16[49152,512]{1,0:T(8,128)(2,1)} %bitcast.99, bf16[512,128]{0,1:T(8,128)(2,1)S(1)} %bitcast.104), kind=kOutput, calls=%fused_computation.103 | convolution fusion | flops 6442450944 | bytes 75628544 | tf_op jit(solution)/shard_map/dot_general | solution.py:60
  1164.2 17.2 %fusion.51 = (f32[8192,128]{1,0:T(8,128)}, f32[8192,128]{1,0:T(8,128)}, f32[8192,128]{1,0:T(8,128)}, f32[8192,128]{1,0:T(8,128)}, f32[8192,128]{1,0:T(8,128)}, /*index=5*/f32[8192,128]{1,0:T(8,128)}) fusion(f32[49152,128]{1,0:T(8,128)} %fusion.54), kind=kLoop, calls=%fused_computation.100 | loop fusion | bytes 50331648 | tf_op jit(solution)/shard_map/slice | solution.py:72
  1187.0 8.1 squeeze.21
  1200.8 7.8 squeeze.20
  1214.2 7.9 squeeze.19
  1227.7 7.8 squeeze.18
  1241.2 7.9 squeeze.17
  1254.7 7.8 squeeze.16
  1262.6 22.6 %multiply_add_fusion = f32[128,64,2,64]{1,0,3,2:T(8,128)} fusion(f32[128,64,2,64]{1,0,3,2:T(8,128)} %squeeze.21, f32[128,64,2,64]{1,0,3,2:T(8,128)} %squeeze.20, f32[128,64,2,64]{1,0,3,2:T(8,128)} %squeeze.19, f32[128,64,2,64]{1,0,3,2:T(8,128)} %squeeze.18, f32[128,64,2,64]{1,0,3,2:T(8,128)} %squeeze.17, f32[128,64,2,64]{1,0,3,2:T(8,128)} %squeeze.16, ...), kind=kLoop, calls=%fused_computation.24 | loop fusion | flops 11534336 | bytes 29361664 | tf_op jit(solution)/shard_map/add | solution.py:74
  1285.3 19.8 %fusion.21 = (f32[64]{0:T(128)S(1)}, f32[64]{0:T(128)S(1)}) fusion(f32[128,64,2,64]{1,0,3,2:T(8,128)} %multiply_add_fusion, f32[64,64]{0,1:T(8,128)S(1)} %copy-done.1, f32[128,64]{0,1:T(8,128)S(1)} %copy-done.2), kind=kLoop, calls=%fused_computation.36 | loop fusion | flops 4718464 | bytes 4243968 | tf_op jit(solution)/shard_map/reduce_sum | solution.py:84
  1305.4 19.1 %all-reduce = f32[8,2,8]{2,1,0:T(2,128)S(1)} all-reduce(f32[8,2,8]{2,1,0:T(2,128)S(1)} %copy.57), channel_id=2, replica_groups=mesh['row'=4,'col'=8] {'col'}, use_global_device_ids=true, to_apply=%region_2.3.clone | all-reduce | flops 128 | bytes 1024
  (67 shorter events, 65.3 us)
Async XLA Ops:
  728.1 7.4 copy-start.12
  728.1 7.5 copy-start.11
  728.1 7.6 copy-start.9
  728.1 8.5 copy-start.13
  728.1 196.0 %all-to-all-start.1 = ((bf16[4,3,44,64,2,128]{5,3,4,2,1,0:T(8,128)(2,1)}), bf16[4,3,44,64,2,128]{5,3,4,2,1,0:T(8,128)(2,1)}, u32[]{:S(2)}, u32[]{:S(2)}) async-start(bf16[4,3,44,64,2,128]{5,3,4,2,1,0:T(8,128)(2,1)} %pad_maximum_fusion), calls=%async_computation.1 | async-start | bytes 34603008 | tf_op jit(solution)/shard_map/all_to_all | solution.py:105
  1088.7 45.5 %copy-start = (bf16[512,2,64]{0,2,1:T(8,128)(2,1)S(1)}, bf16[512,2,64]{0,2,1:T(8,128)(2,1)}, u32[]{:S(2)}) copy-start(bf16[512,2,64]{0,2,1:T(8,128)(2,1)} %pad_maximum_fusion.4) | copy-start | bytes 393220
  1249.0 13.5 %copy-start.3 = (f32[64]{0:T(128)S(1)}, f32[64]{0:T(128)}, u32[]{:S(2)}) copy-start(f32[64]{0:T(128)} %get-tuple-element.31) | copy-start | bytes 772
  1249.0 13.5 %copy-start.4 = (f32[64]{0:T(128)S(1)}, f32[64]{0:T(128)}, u32[]{:S(2)}) copy-start(f32[64]{0:T(128)} %get-tuple-element.32) | copy-start | bytes 772
  1249.0 13.5 %copy-start.5 = (f32[64]{0:T(128)S(1)}, f32[64]{0:T(128)}, u32[]{:S(2)}) copy-start(f32[64]{0:T(128)} %get-tuple-element.33) | copy-start | bytes 772
  1249.0 13.5 %copy-start.6 = (f32[64]{0:T(128)S(1)}, f32[64]{0:T(128)}, u32[]{:S(2)}) copy-start(f32[64]{0:T(128)} %get-tuple-element.38) | copy-start | bytes 772
  1249.0 13.5 %copy-start.7 = (f32[64]{0:T(128)S(1)}, f32[64]{0:T(128)}, u32[]{:S(2)}) copy-start(f32[64]{0:T(128)} %get-tuple-element.39) | copy-start | bytes 772
  1249.1 13.5 %copy-start.8 = (f32[64]{0:T(128)S(1)}, f32[64]{0:T(128)}, u32[]{:S(2)}) copy-start(f32[64]{0:T(128)} %get-tuple-element.40) | copy-start | bytes 772
  1262.6 22.7 %copy-start.1 = (f32[64,64]{0,1:T(8,128)S(1)}, f32[64,64]{0,1:T(8,128)}, u32[]{:S(2)}) copy-start(f32[64,64]{0,1:T(8,128)} %multiply_multiply_fusion.1) | copy-start | bytes 49156
  1262.6 22.7 %copy-start.2 = (f32[128,64]{0,1:T(8,128)S(1)}, f32[128,64]{0,1:T(8,128)}, u32[]{:S(2)}) copy-start(f32[128,64]{0,1:T(8,128)} %multiply_multiply_fusion.2) | copy-start | bytes 98308
  1262.6 42.6 %copy-start.10 = (f32[8]{0:T(128)S(1)}, f32[8]{0:T(128)}, u32[]{:S(2)}) copy-start(f32[8]{0:T(128)} %mul.534) | copy-start | bytes 100
